TPU v7x, 512 devices: a whole 4x4x16 slice. The times are simulated.
512 devices in a mesh: dp: 4 (over y_lo, core), tp: 128 (over z, x, y_hi).
Axes of the slice: x: 4, y: 4 (y_hi: 2, y_lo: 2; y = y_hi * 2 + y_lo), z: 16, core: 2. Of those that a mesh axis runs over, the one named last changes fastest.
Arguments:
- inputs: bfloat16 [4, 128, 8192], P('dp', 'tp'), may hold values from -134 to 134, as said below
- norm_gain: float32 [8192], replicated, may hold values from 0.1 to 1.9
- gate_grad: bfloat16 [4, 128, 16384], P('dp', None, 'tp'), may hold values from -36 to 36
- up_grad: bfloat16 [4, 128, 16384], P('dp', None, 'tp'), may hold values from -36 to 36
- gate_weight: bfloat16 [8192, 16384], P(None, 'tp'), may hold values from -0.046875 to 0.046875
- up_weight: bfloat16 [8192, 16384], P(None, 'tp'), may hold values from -0.046875 to 0.046875
Outputs:
- input_grad: bfloat16 [4, 128, 8192], P('dp', 'tp')
- gain_grad: float32 [8192], replicated
Inputs may be any that keep to these rules, and one draw needn't show every extreme that they name: `inputs`: activations with token and feature scales.
All inputs are finite; a program needn't handle non-finite values.
Results may differ from a plain program's by a relative error of at most 0.00165.
Values may be sent and summed in bfloat16 or wider, within the bound.
A program may use at most 64 MiB of HBM per device.

v0:
```python
import jax
import jax.numpy as jnp
from jax import lax
from jax.sharding import Mesh
from jax.sharding import PartitionSpec as P

DP_TP = ("dp_0", "dp_1", "tp_0", "tp_1", "tp_2")
TP = ("tp_0", "tp_1", "tp_2")
DP = ("dp_0", "dp_1")
epsilon = 1e-05


def over_axes(x, axes):
    for axis in axes:
        x = lax.psum(x, axis)
    return x


def split_up(x, dim, count):
    before, after = (x.shape[:dim], x.shape[dim + 1 :])
    return jnp.moveaxis(x.reshape(*before, count, -1, *after), dim, 0)


def sent_and_summed(x, axis, dim):
    tiles = split_up(x, dim, lax.axis_size(axis))
    arrived = lax.all_to_all(tiles, axis, split_axis=0, concat_axis=0, tiled=True)
    return arrived.sum(axis=0)


def sum_by_axis(x, axes, dim):
    far, near = axes
    tiles = split_up(x, dim, lax.axis_size(far))
    nearer = sent_and_summed(tiles, near, dim + 1)
    arrived = lax.all_to_all(nearer, far, split_axis=0, concat_axis=0, tiled=True)
    return arrived.sum(axis=0)


def normalize(values):
    inv_rms = lax.rsqrt(jnp.mean(values * values, axis=-1, keepdims=True) + epsilon)
    return (inv_rms, values * inv_rms)


def total_gain(partial_gain):
    return over_axes(partial_gain, DP_TP)


def per_device(inputs, norm_gain, gate_grad, up_grad, gate_weight, up_weight):
    cot_gate = gate_grad[0]
    cot_up = up_grad[0]
    dims = (((1,), (1,)), ((), ()))
    local_rows = inputs[0].astype(jnp.float32)
    inv_rms, normed = normalize(local_rows)
    result = lax.dot_general(cot_gate, gate_weight, dims, preferred_element_type=jnp.float32)
    row_grad = sum_by_axis(
        result + lax.dot_general(cot_up, up_weight, dims, preferred_element_type=jnp.float32),
        (("tp_0", "tp_1"), "tp_2"),
        0,
    )
    gain_grad = total_gain(jnp.sum(row_grad * normed, axis=0))
    scaled = row_grad * norm_gain
    inner = jnp.mean(scaled * normed, axis=-1, keepdims=True)
    input_grad = (inv_rms * (scaled - normed * inner)).astype(jnp.bfloat16)
    return (input_grad[None], gain_grad)


def solution(mesh):
    finer = Mesh(mesh.devices.reshape(2, 2, 16, 4, 2), ("dp_0", "dp_1", "tp_0", "tp_1", "tp_2"))
    return jax.shard_map(
        per_device,
        mesh=finer,
        in_specs=(P(DP, TP, None), P(), P(DP, None, TP), P(DP, None, TP), P(None, TP), P(None, TP)),
        out_specs=(P(DP, TP, None), P()),
        check_vma=False,
    )
```

profile of v0, /device:TPU:16, one launch (start us, length us, event | category | flops | bytes accessed | tf_op | source)
XLA Modules:
  0.0 293.2 jit_solution(13925737791889651203)
XLA Ops:
  0.6 0.0 copy-start
  0.6 0.0 copy-start.1
  0.7 0.0 copy-start.3
  0.7 1.6 copy-done
  2.2 1.5 fusion.1
  3.7 0.0 copy-done.1
  3.7 0.0 copy-done.3
  3.7 2.6 convolution_add_fusion
  6.4 5.8 %reshape_reshape.3 = f32[64,2,1,8192]{3,1,0,2:T(2,128)} reshape(f32[128,8192]{1,0:T(8,128)} %convolution_add_fusion) | data formatting | bytes 8388608 | tf_op jit(solution)/shard_map/reshape;reshape | solution.py:21
  12.2 4.6 %copy.10 = f32[64,2,1,8192]{3,0,2,1:T(8,128)S(1)} copy(f32[64,2,1,8192]{3,1,0,2:T(2,128)} %reshape_reshape.3) | data formatting | bytes 8388608 | tf_op jit(solution)/shard_map/reshape;reshape | solution.py:21
  16.8 50.2 %all_to_all.10 = f32[2,64,1,8192]{3,1,2,0:T(8,128)} all-to-all(f32[2,64,1,8192]{3,1,2,0:T(8,128)S(1)} %bitcast.12), channel_id=1, replica_groups=mesh['dp_0'=2,'dp_1'=2,'tp_0'=16,'tp_1'=4,'tp_2'=2] {'tp_2'}, dimensions={0} | all-to-all | bytes 8388608 | tf_op jit(solution)/shard_map/all_to_all | solution.py:26
  67.0 4.0 %reduce_sum.43 = f32[64,8192]{1,0:T(8,128)} reduce(f32[2,64,1,8192]{3,1,2,0:T(8,128)} %all_to_all.10, f32[]{:T(128)} %constant.8.clone.1), dimensions={0,2}, to_apply=%region_1.0 | reduce | flops 524288 | bytes 6291460 | tf_op jit(solution)/shard_map/reduce_sum | solution.py:27
  71.0 5.3 %reduce_sum.44 = f32[64,1,8192]{2,1,0:T(1,128)} reshape(f32[64,8192]{1,0:T(8,128)} %reduce_sum.43) | data formatting | bytes 4194304 | tf_op jit(solution)/shard_map/reduce_sum | solution.py:27
  76.3 0.0 copy-start.2
  76.3 19.0 %all-to-all-start.1 = ((f32[64,1,8192]{2,1,0:T(1,128)}), f32[64,1,8192]{2,1,0:T(1,128)}, u32[]{:S(2)}, u32[]{:S(2)}) async-start(f32[64,1,8192]{2,1,0:T(1,128)} %reduce_sum.44), calls=%async_computation.1 | async-start | bytes 4194304 | tf_op jit(solution)/shard_map/all_to_all | solution.py:34
  95.3 0.0 copy-done.2
  95.3 0.0 copy-start.4
  95.3 0.7 multiply_reduce_fusion.1
  96.7 97.8 %all-to-all-done.1 = f32[64,1,8192]{2,1,0:T(1,128)} async-done(((f32[64,1,8192]{2,1,0:T(1,128)}), f32[64,1,8192]{2,1,0:T(1,128)}, u32[]{:S(2)}, u32[]{:S(2)}) %all-to-all-start.1) | async-done | bytes 2097184 | tf_op jit(solution)/shard_map/all_to_all | solution.py:34
  194.5 3.4 %reduce_sum.45 = f32[8192]{0:T(1024)S(1)} reduce(f32[64,1,8192]{2,1,0:T(1,128)} %all-to-all-done.1, f32[]{:T(128)} %constant.8.clone.1), dimensions={0,1}, to_apply=%region_2.0 | reduce | flops 516096 | bytes 2129924 | tf_op jit(solution)/shard_map/reduce_sum | solution.py:35
  197.9 0.0 copy-done.4
  197.9 0.6 multiply_reduce_fusion
  199.2 0.6 broadcast_in_dim.2
  199.8 9.0 %psum.35 = f32[8192]{0:T(1024)S(1)} all-reduce(f32[8192]{0:T(1024)S(1)} %get-tuple-element.4), channel_id=1, replica_groups=mesh['dp_0'=2,'dp_1'=2,'tp_0'=16,'tp_1'=4,'tp_2'=2] {'dp_0'}, use_global_device_ids=true, to_apply=%region_4.0 | all-reduce | flops 8192 | bytes 65536 | tf_op jit(solution)/shard_map/psum | solution.py:15
  208.8 3.4 %psum.36 = f32[8192]{0:T(1024)S(1)} all-reduce(f32[8192]{0:T(1024)S(1)} %psum.35), channel_id=1, replica_groups=mesh['dp_0'=2,'dp_1'=2,'tp_0'=16,'tp_1'=4,'tp_2'=2] {'dp_1'}, use_global_device_ids=true, to_apply=%region_5.0 | all-reduce | flops 8192 | bytes 65536 | tf_op jit(solution)/shard_map/psum | solution.py:15
  212.3 52.7 %psum.37 = f32[8192]{0:T(1024)S(1)} all-reduce(f32[8192]{0:T(1024)S(1)} %psum.36), channel_id=1, replica_groups=mesh['dp_0'=2,'dp_1'=2,'tp_0'=16,'tp_1'=4,'tp_2'=2] {'tp_0'}, use_global_device_ids=true, to_apply=%region_6.0 | all-reduce | flops 8192 | bytes 65536 | tf_op jit(solution)/shard_map/psum | solution.py:15
  264.9 17.0 %psum.38 = f32[8192]{0:T(1024)S(1)} all-reduce(f32[8192]{0:T(1024)S(1)} %psum.37), channel_id=1, replica_groups=mesh['dp_0'=2,'dp_1'=2,'tp_0'=16,'tp_1'=4,'tp_2'=2] {'tp_1'}, use_global_device_ids=true, to_apply=%region_7.0 | all-reduce | flops 8192 | bytes 65536 | tf_op jit(solution)/shard_map/psum | solution.py:15
  281.9 11.3 %psum.39 = f32[8192]{0:T(1024)} all-reduce(f32[8192]{0:T(1024)S(1)} %psum.38), channel_id=1, replica_groups=mesh['dp_0'=2,'dp_1'=2,'tp_0'=16,'tp_1'=4,'tp_2'=2] {'tp_2'}, use_global_device_ids=true, to_apply=%region_8.0 | all-reduce | flops 8192 | bytes 65536 | tf_op jit(solution)/shard_map/psum | solution.py:15
  (2 shorter events, 0.0 us)
Async XLA Ops:
  0.6 1.6 copy-start
  0.6 3.1 %copy-start.1 = (bf16[8192,128]{1,0:T(8,128)(2,1)S(1)}, bf16[8192,128]{1,0:T(8,128)(2,1)}, u32[]{:S(2)}) copy-start(bf16[8192,128]{1,0:T(8,128)(2,1)} %param.11) | copy-start | bytes 6291460
  0.7 3.1 %copy-start.3 = (bf16[1,128,128]{2,1,0:T(8,128)(2,1)S(1)}, bf16[1,128,128]{2,1,0:T(8,128)(2,1)}, u32[]{:S(2)}) copy-start(bf16[1,128,128]{2,1,0:T(8,128)(2,1)} %param.9) | copy-start | bytes 98308
  76.3 19.0 %copy-start.2 = (bf16[1,1,8192]{2,1,0:T(2,128)(2,1)S(1)}, bf16[1,1,8192]{2,1,0:T(2,128)(2,1)}, u32[]{:S(2)}) copy-start(bf16[1,1,8192]{2,1,0:T(2,128)(2,1)} %param.6) | copy-start | bytes 49156
  76.3 118.2 %all-to-all-start.1 = ((f32[64,1,8192]{2,1,0:T(1,128)}), f32[64,1,8192]{2,1,0:T(1,128)}, u32[]{:S(2)}, u32[]{:S(2)}) async-start(f32[64,1,8192]{2,1,0:T(1,128)} %reduce_sum.44), calls=%async_computation.1 | async-start | bytes 4194304 | tf_op jit(solution)/shard_map/all_to_all | solution.py:34
  95.3 102.6 %copy-start.4 = (f32[8192]{0:T(1024)S(1)}, f32[8192]{0:T(1024)}, u32[]{:S(2)}) copy-start(f32[8192]{0:T(1024)} %param.7) | copy-start | bytes 98308
where the time goes:
time: 294 us; the launch traced here: 293 us
  blocking collectives  144 us (49%)
  waiting for transfers between devices  97.8 us (33%)
  starting transfers between devices  19 us (6%)
  local copies, waits for them, and re-layouts  17.9 us (6%)
  other arithmetic  8.7 us (3%)
  matrix products  4.1 us (1%)
    all_to_all x1, waiting for transfers between devices, sum_by_axis(): lax.all_to_all(nearer, far, split_axis=0, concat_axis=0, tiled=True)  97.8 us
    psum x5, blocking collectives, over_axes(): x = lax.psum(x, axis)  93.4 us
    all_to_all x1, blocking collectives, sent_and_summed(): lax.all_to_all(tiles, axis, split_axis=0, concat_axis=0, tiled=True)  50.2 us
    all_to_all x1, starting transfers between devices, sum_by_axis(): lax.all_to_all(nearer, far, split_axis=0, concat_axis=0, tiled=True)  19 us
    another operation x2, local copies, waits for them, and re-layouts, split_up(): return jnp.moveaxis(x.reshape(*before, count, -1, *after), dim, 0)  10.4 us
  transfers between devices with their start and end apart: 1, of which 1 were waited for; matrix products, arithmetic and copies ran while one was open for 0% of the time, Pallas kernels for 0%

commit v1 on v0

--- a/solution.py
+++ b/solution.py
@@ -12,7 +12,7 @@
 
 def over_axes(x, axes):
     for axis in axes:
-        x = lax.psum(x, axis)
+        x = jnp.sum(lax.all_gather(x, axis), axis=0)
     return x
 
 

time: 294 us -> 259 us (0.88)
  the two profiles are of different devices: /device:TPU:16 before, /device:TPU:8 now
where the time goes in v1:
time: 259 us; the launch traced here: 258 us
  blocking collectives  107 us (41%)
  waiting for transfers between devices  97.8 us (38%)
  starting transfers between devices  19 us (7%)
  local copies, waits for them, and re-layouts  18.2 us (7%)
  other arithmetic  9.74 us (4%)
  matrix products  4.1 us (2%)
    all_to_all x1, waiting for transfers between devices, sum_by_axis(): lax.all_to_all(nearer, far, split_axis=0, concat_axis=0, tiled=True)  97.8 us
    all_gather x5, blocking collectives, over_axes(): x = jnp.sum(lax.all_gather(x, axis), axis=0)  54.1 us
    all_to_all x1, blocking collectives, sent_and_summed(): lax.all_to_all(tiles, axis, split_axis=0, concat_axis=0, tiled=True)  52.9 us
    all_to_all x1, starting transfers between devices, sum_by_axis(): lax.all_to_all(nearer, far, split_axis=0, concat_axis=0, tiled=True)  19 us
    another operation x2, local copies, waits for them, and re-layouts, split_up(): return jnp.moveaxis(x.reshape(*before, count, -1, *after), dim, 0)  10.4 us
    reduce_sum x1, local copies, waits for them, and re-layouts, sent_and_summed(): return arrived.sum(axis=0)  5.29 us
  transfers between devices with their start and end apart: 1, of which 1 were waited for; matrix products, arithmetic and copies ran while one was open for 0% of the time, Pallas kernels for 0%

profile of v1, /device:TPU:8, one launch (start us, length us, event | category | flops | bytes accessed | tf_op | source)
XLA Modules:
  0.0 257.9 jit_solution(16385915251545719793)
XLA Ops:
  0.6 0.0 copy-start
  0.6 0.0 copy-start.1
  0.7 0.0 copy-start.3
  0.7 1.6 copy-done
  2.2 1.5 fusion.2
  3.7 0.0 copy-done.1
  3.7 0.0 copy-done.3
  3.7 2.6 %convolution_add_fusion = f32[128,8192]{1,0:T(8,128)} fusion(f32[128,8192]{1,0:T(8,128)S(1)} %fusion.2, bf16[8192,128]{1,0:T(8,128)(2,1)S(1)} %copy-done.1, bf16[1,128,128]{2,1,0:T(8,128)(2,1)S(1)} %copy-done.3), kind=kOutput, calls=%fused_computation | convolution fusion | flops 269484032 | bytes 10518528 | tf_op jit(solution)/shard_map/dot_general | solution.py:55
  6.4 5.8 %reshape_reshape.3 = f32[64,2,1,8192]{3,1,0,2:T(2,128)} reshape(f32[128,8192]{1,0:T(8,128)} %convolution_add_fusion) | data formatting | bytes 8388608 | tf_op jit(solution)/shard_map/reshape;reshape | solution.py:21
  12.2 4.6 %copy.11 = f32[64,2,1,8192]{3,0,2,1:T(8,128)S(1)} copy(f32[64,2,1,8192]{3,1,0,2:T(2,128)} %reshape_reshape.3) | data formatting | bytes 8388608 | tf_op jit(solution)/shard_map/reshape;reshape | solution.py:21
  16.8 52.9 %all_to_all.10 = f32[2,64,1,8192]{3,1,2,0:T(8,128)} all-to-all(f32[2,64,1,8192]{3,1,2,0:T(8,128)S(1)} %bitcast.19), channel_id=1, replica_groups=mesh['dp_0'=2,'dp_1'=2,'tp_0'=16,'tp_1'=4,'tp_2'=2] {'tp_2'}, dimensions={0} | all-to-all | bytes 8388608 | tf_op jit(solution)/shard_map/all_to_all | solution.py:26
  69.7 4.0 %reduce_sum.90 = f32[64,8192]{1,0:T(8,128)} reduce(f32[2,64,1,8192]{3,1,2,0:T(8,128)} %all_to_all.10, f32[]{:T(128)} %constant.8.clone.1), dimensions={0,2}, to_apply=%region_1.0 | reduce | flops 524288 | bytes 6291460 | tf_op jit(solution)/shard_map/reduce_sum | solution.py:27
  73.7 5.3 %reduce_sum.91 = f32[64,1,8192]{2,1,0:T(1,128)} reshape(f32[64,8192]{1,0:T(8,128)} %reduce_sum.90) | data formatting | bytes 4194304 | tf_op jit(solution)/shard_map/reduce_sum | solution.py:27
  79.0 0.0 copy-start.2
  79.0 19.0 %all-to-all-start.1 = ((f32[64,1,8192]{2,1,0:T(1,128)}), f32[64,1,8192]{2,1,0:T(1,128)}, u32[]{:S(2)}, u32[]{:S(2)}) async-start(f32[64,1,8192]{2,1,0:T(1,128)} %reduce_sum.91), calls=%async_computation.1 | async-start | bytes 4194304 | tf_op jit(solution)/shard_map/all_to_all | solution.py:34
  97.9 0.0 copy-done.2
  97.9 0.0 copy-start.4
  97.9 0.7 multiply_reduce_fusion.1
  99.3 97.8 %all-to-all-done.1 = f32[64,1,8192]{2,1,0:T(1,128)} async-done(((f32[64,1,8192]{2,1,0:T(1,128)}), f32[64,1,8192]{2,1,0:T(1,128)}, u32[]{:S(2)}, u32[]{:S(2)}) %all-to-all-start.1) | async-done | bytes 2097184 | tf_op jit(solution)/shard_map/all_to_all | solution.py:34
  197.1 3.4 %reduce_sum.92 = f32[8192]{0:T(1024)S(1)} reduce(f32[64,1,8192]{2,1,0:T(1,128)} %all-to-all-done.1, f32[]{:T(128)} %constant.8.clone.1), dimensions={0,1}, to_apply=%region_2.0 | reduce | flops 516096 | bytes 2129924 | tf_op jit(solution)/shard_map/reduce_sum | solution.py:35
  200.5 0.1 fusion
  200.6 0.0 copy-done.4
  200.6 0.6 multiply_reduce_fusion
  201.9 0.6 broadcast_in_dim.2
  202.5 4.6 %all-gather.4 = f32[2,1,8192]{2,1,0:T(1,128)S(1)} all-gather(f32[1,1,8192]{2,1,0:T(1,128)S(1)} %get-tuple-element.2), channel_id=1, replica_groups=mesh['dp_0'=2,'dp_1'=2,'tp_0'=16,'tp_1'=4,'tp_2'=2] {'dp_0'}, dimensions={0}, use_global_device_ids=true | all-gather | bytes 98304 | tf_op jit(solution)/shard_map/all_gather | solution.py:15
  207.1 0.1 reduce_sum.95
  207.2 1.9 all-gather
  209.1 0.1 reduce_sum.96
  209.1 29.3 %all-gather.1 = f32[131072]{0:T(1024)S(1)} all-gather(f32[8192]{0:T(1024)S(1)} %reduce_sum.96), channel_id=3, replica_groups=mesh['dp_0'=2,'dp_1'=2,'tp_0'=16,'tp_1'=4,'tp_2'=2] {'tp_0'}, dimensions={0}, use_global_device_ids=true | all-gather | bytes 557056 | tf_op jit(solution)/shard_map/all_gather | solution.py:15
  238.4 0.1 reshape.76
  238.5 0.1 reduce_sum.97
  238.6 12.3 %all-gather.2 = f32[32768]{0:T(1024)S(1)} all-gather(f32[8192]{0:T(1024)S(1)} %reduce_sum.97), channel_id=4, replica_groups=mesh['dp_0'=2,'dp_1'=2,'tp_0'=16,'tp_1'=4,'tp_2'=2] {'tp_1'}, dimensions={0}, use_global_device_ids=true | all-gather | bytes 163840 | tf_op jit(solution)/shard_map/all_gather | solution.py:15
  251.0 0.1 reduce_sum.98
  251.1 6.1 %all-gather.3 = f32[16384]{0:T(1024)S(1)} all-gather(f32[8192]{0:T(1024)S(1)} %reduce_sum.98), channel_id=5, replica_groups=mesh['dp_0'=2,'dp_1'=2,'tp_0'=16,'tp_1'=4,'tp_2'=2] {'tp_2'}, dimensions={0}, use_global_device_ids=true | all-gather | bytes 98304 | tf_op jit(solution)/shard_map/all_gather | solution.py:15
  257.2 0.7 reduce_sum.99
  (4 shorter events, 0.1 us)
Async XLA Ops:
  0.6 1.6 copy-start
  0.6 3.1 %copy-start.1 = (bf16[8192,128]{1,0:T(8,128)(2,1)S(1)}, bf16[8192,128]{1,0:T(8,128)(2,1)}, u32[]{:S(2)}) copy-start(bf16[8192,128]{1,0:T(8,128)(2,1)} %param.11) | copy-start | bytes 6291460
  0.7 3.1 %copy-start.3 = (bf16[1,128,128]{2,1,0:T(8,128)(2,1)S(1)}, bf16[1,128,128]{2,1,0:T(8,128)(2,1)}, u32[]{:S(2)}) copy-start(bf16[1,128,128]{2,1,0:T(8,128)(2,1)} %param.9) | copy-start | bytes 98308
  79.0 19.0 %copy-start.2 = (bf16[1,1,8192]{2,1,0:T(2,128)(2,1)S(1)}, bf16[1,1,8192]{2,1,0:T(2,128)(2,1)}, u32[]{:S(2)}) copy-start(bf16[1,1,8192]{2,1,0:T(2,128)(2,1)} %param.6) | copy-start | bytes 49156
  79.0 118.2 %all-to-all-start.1 = ((f32[64,1,8192]{2,1,0:T(1,128)}), f32[64,1,8192]{2,1,0:T(1,128)}, u32[]{:S(2)}, u32[]{:S(2)}) async-start(f32[64,1,8192]{2,1,0:T(1,128)} %reduce_sum.91), calls=%async_computation.1 | async-start | bytes 4194304 | tf_op jit(solution)/shard_map/all_to_all | solution.py:34
  97.9 102.7 %copy-start.4 = (f32[8192]{0:T(1024)S(1)}, f32[8192]{0:T(1024)}, u32[]{:S(2)}) copy-start(f32[8192]{0:T(1024)} %param.7) | copy-start | bytes 98308
